TPU v7x, 32 devices: a whole 2x2x4 slice. The times are simulated.
32 devices in a mesh: dp: 4 (over y, core), seq: 2 (over x), head: 4 (over z).
Axes of the slice: x: 2, y: 2, z: 4, core: 2. Of those that a mesh axis runs over, the one named last changes fastest.
Arguments:
- queries: bfloat16 [4, 512, 1536], P('dp', 'seq', 'head'), may hold values from -160 to 160
- key_cache: bfloat16 [4, 512, 512], P('dp', 'seq', 'head'), may hold values from -7 to 7
- value_cache: bfloat16 [4, 512, 512], P('dp', 'seq', 'head'), may hold values from -6 to 6
- out_grad: bfloat16 [4, 512, 1536], P('dp', 'seq', 'head'), may hold values from -6 to 6
- doc_ids: int32 [4, 512], P('dp', 'seq'), may hold values from 0 to 1, never falling along the last dimension, each value on 1 to 511 neighbouring positions
- layer_input: bfloat16 [4, 512, 3072], P('dp', ('seq', 'head')), may hold values from -6 to 6
- key_proj: bfloat16 [3072, 512], P(None, 'head'), may hold values from -0.109375 to 0.109375
- value_proj: bfloat16 [3072, 512], P(None, 'head'), may hold values from -0.109375 to 0.109375
Outputs:
- query_grad: bfloat16 [4, 512, 1536], P('dp', 'seq', 'head')
- input_grad: bfloat16 [4, 512, 3072], P('dp', ('seq', 'head'))
- grad_keyproj: float32 [3072, 512], P(None, 'head')
- grad_valueproj: float32 [3072, 512], P(None, 'head')
Inputs may be any that keep to these rules, and one draw needn't show every extreme that they name: `doc_ids`: document numbers never fall along a sequence; a document spans 1 to 511 positions.
All inputs are finite; a program needn't handle non-finite values.
Results may differ from a plain program's by a relative error of at most 0.02.
Values may be sent and summed in bfloat16 or wider, within the bound.
No kernel may reach another device: no remote copies, remote signals or barrier semaphores. Data moves between devices by JAX's collectives and lax.ppermute only.
A program may use at most 64 MiB of HBM per device.

v0:
```python
import jax
import jax.numpy as jnp
from jax import lax
from jax.sharding import PartitionSpec as P

D = 3072
HD = 128
GROUP = 3
NEG_FILL = -1e30


def shards(queries, key_cache, value_cache, out_grad, doc_ids, layer_input, key_proj, value_proj):
    rows_query = queries.shape[1]
    col_width = key_cache.shape[2]
    kv_heads = col_width // HD
    cycle_size = lax.axis_size("seq")
    head_count = lax.axis_size("head")
    own_index = lax.axis_index("seq")
    score_scale = HD ** (-0.5)
    query_four = queries[0].reshape(rows_query, kv_heads, GROUP, HD)
    grad_four = out_grad[0].reshape(rows_query, kv_heads, GROUP, HD)
    own_blocks = jnp.stack([key_cache[0], value_cache[0]])
    all_docs = lax.all_gather(doc_ids, "seq", axis=1, tiled=True)[0]
    query_doc = doc_ids[0]
    query_pos = own_index * rows_query + lax.iota(jnp.int32, rows_query)
    last_pos = own_index * rows_query + rows_query - 1

    def block_scores(kv_piece, row_start):
        row_total = kv_piece.shape[1]
        key_block = kv_piece[0].reshape(row_total, kv_heads, HD)
        value_block = kv_piece[1].reshape(row_total, kv_heads, HD)
        key_pos = row_start + lax.iota(jnp.int32, row_total)
        key_doc = lax.dynamic_slice_in_dim(all_docs, row_start, row_total)
        allowed = (key_pos[None, :] <= query_pos[:, None]) & (
            key_doc[None, :] == query_doc[:, None]
        )
        scores = (
            jnp.einsum("ihge,jhe->hgij", query_four, key_block, preferred_element_type=jnp.float32)
            * score_scale
        )
        masked = jnp.where(allowed, scores, NEG_FILL)
        weight_grad = jnp.einsum(
            "ihge,jhe->hgij", grad_four, value_block, preferred_element_type=jnp.float32
        )
        return (key_block, allowed, masked, weight_grad)

    def stats_block(state_in, kv_piece, row_start):
        row_top, row_sum, row_acc = state_in
        key_block, allowed, masked, weight_grad = block_scores(kv_piece, row_start)
        new_top = jnp.maximum(row_top, jnp.max(masked, axis=-1))
        weights = jnp.where(allowed, jnp.exp(masked - new_top[..., None]), 0.0)
        decay = jnp.exp(row_top - new_top)
        return (
            new_top,
            row_sum * decay + jnp.sum(weights, axis=-1),
            row_acc * decay + jnp.sum(weights * weight_grad, axis=-1),
        )

    def stats_fold(state_in, kv_piece, row_start):
        row_total = kv_piece.shape[1]
        sub_rows = min(row_total, rows_query)

        def one_part(part_num, state_mid):
            part_start = row_start + part_num * sub_rows
            sub_piece = kv_piece
            return lax.cond(
                part_start <= last_pos,
                lambda: stats_block(state_mid, sub_piece, part_start),
                lambda: state_mid,
            )

        return lax.fori_loop(0, row_total // sub_rows, one_part, state_in)

    stat_shape = (kv_heads, GROUP, rows_query)
    stats_init = (
        jnp.full(stat_shape, NEG_FILL, jnp.float32),
        jnp.zeros(stat_shape, jnp.float32),
        jnp.zeros(stat_shape, jnp.float32),
    )
    all_blocks = lax.all_gather(own_blocks, "seq", axis=1, tiled=True)
    row_top, row_sum, row_acc = lax.fori_loop(
        0,
        cycle_size,
        lambda block_num, state_mid: stats_fold(
            state_mid,
            lax.dynamic_slice_in_dim(all_blocks, block_num * rows_query, rows_query, 1),
            block_num * rows_query,
        ),
        stats_init,
    )
    log_total = row_top + jnp.log(row_sum)
    row_delta = row_acc / row_sum

    def grad_block(kv_piece, row_start):
        row_total = kv_piece.shape[1]
        key_block, allowed, masked, weight_grad = block_scores(kv_piece, row_start)
        weights = jnp.where(allowed, jnp.exp(masked - log_total[..., None]), 0.0)
        score_grad = (weights * (weight_grad - row_delta[..., None]) * score_scale).astype(
            jnp.bfloat16
        )
        weights_low = weights.astype(jnp.bfloat16)
        query_add = jnp.einsum(
            "hgij,jhe->ihge", score_grad, key_block, preferred_element_type=jnp.float32
        )
        key_add = jnp.einsum(
            "hgij,ihge->jhe", score_grad, query_four, preferred_element_type=jnp.float32
        )
        value_add = jnp.einsum(
            "hgij,ihge->jhe", weights_low, grad_four, preferred_element_type=jnp.float32
        )
        return (
            query_add,
            jnp.stack(
                [key_add.reshape(row_total, col_width), value_add.reshape(row_total, col_width)]
            ),
        )

    zero_query = jnp.zeros((rows_query, kv_heads, GROUP, HD), jnp.float32)

    def guarded(kv_piece, row_start):
        return lax.cond(
            row_start <= last_pos,
            lambda: grad_block(kv_piece, row_start),
            lambda: (zero_query, jnp.zeros(kv_piece.shape, jnp.float32)),
        )

    def gathered_turn(block_num, state_mid):
        grad_terms, query_sum = state_mid
        row_start = block_num * rows_query
        kv_piece = lax.dynamic_slice_in_dim(all_blocks, row_start, rows_query, 1)
        query_add, kv_add = guarded(kv_piece, row_start)
        return (
            lax.dynamic_update_slice_in_dim(grad_terms, kv_add, row_start, 1),
            query_sum + query_add,
        )

    terms_init = jnp.zeros(all_blocks.shape, jnp.float32)
    grad_terms, query_sum = lax.fori_loop(0, cycle_size, gathered_turn, (terms_init, zero_query))
    kv_grads = lax.psum_scatter(
        grad_terms.astype(jnp.bfloat16), "seq", scatter_dimension=1, tiled=True
    )
    query_grad = query_sum.astype(jnp.bfloat16).reshape(1, rows_query, kv_heads * GROUP * HD)
    input_rows = rows_query // head_count
    contract_cols = (((1,), (1,)), ((), ()))
    sub_grads = kv_grads
    key_term = lax.dot_general(
        sub_grads[0], key_proj, contract_cols, preferred_element_type=jnp.float32
    )
    value_term = lax.dot_general(
        sub_grads[1], value_proj, contract_cols, preferred_element_type=jnp.float32
    )
    input_sum = lax.psum_scatter(
        (key_term + value_term).astype(jnp.bfloat16), "head", scatter_dimension=0, tiled=True
    )
    input_grad = input_sum.reshape(1, input_rows, D)
    contract_rows = (((0,), (0,)), ((), ()))
    input_piece = lax.all_gather(layer_input[0], "head", axis=0, tiled=True)
    row_total = input_piece.shape[0]
    sub_grads = kv_grads
    key_part = lax.dot_general(
        input_piece, sub_grads[0], contract_rows, preferred_element_type=jnp.float32
    )
    value_part = lax.dot_general(
        input_piece, sub_grads[1], contract_rows, preferred_element_type=jnp.float32
    )
    grad_keyproj, grad_valueproj = (
        lax.psum(key_part.astype(jnp.bfloat16), ("dp", "seq")).astype(jnp.float32),
        lax.psum(value_part.astype(jnp.bfloat16), ("dp", "seq")).astype(jnp.float32),
    )
    return (query_grad, input_grad, grad_keyproj, grad_valueproj)


def solution(mesh):
    return jax.shard_map(
        shards,
        mesh=mesh,
        in_specs=(
            P("dp", "seq", "head"),
            P("dp", "seq", "head"),
            P("dp", "seq", "head"),
            P("dp", "seq", "head"),
            P("dp", "seq"),
            P("dp", ("seq", "head"), None),
            P(None, "head"),
            P(None, "head"),
        ),
        out_specs=(
            P("dp", "seq", "head"),
            P("dp", ("seq", "head"), None),
            P(None, "head"),
            P(None, "head"),
        ),
        check_vma=False,
    )
```

profile of v0, /device:TPU:0, one launch (start us, length us, event | category | flops | bytes accessed | tf_op | source)
XLA Modules:
  0.0 143.1 jit_solution(12248398313771703250)
XLA Ops:
  8.1 1.0 pad_maximum_fusion.1
  9.1 7.1 %all_gather.9 = bf16[2,512,128]{2,1,0:T(8,128)(2,1)S(1)} all-gather(bf16[2,256,128]{2,1,0:T(8,128)(2,1)S(1)} %pad_maximum_fusion.1), channel_id=1, replica_groups=mesh['dp'=4,'seq'=2,'head'=4] {'seq'}, dimensions={1}, use_global_device_ids=true | all-gather | bytes 393216 | tf_op jit(solution)/shard_map/all_gather | solution.py:80
  16.2 4.4 %all_gather.10 = s32[1,512]{1,0:T(1,128)S(1)} all-gather(s32[1,256]{1,0:T(1,128)} %param.20), channel_id=1, replica_groups=mesh['dp'=4,'seq'=2,'head'=4] {'seq'}, dimensions={1}, use_global_device_ids=true | all-gather | bytes 3072 | tf_op jit(solution)/shard_map/all_gather | solution.py:23
  20.6 1.1 copy.19
  21.7 0.2 copy.23
  21.9 0.1 copy.20
  22.0 0.2 copy.22
  22.2 1.2 while.49
  22.3 1.1 conditional.6
  22.5 0.3 fusion.38
  22.9 0.3 fusion.7
  23.2 0.2 fusion.8
  23.5 2.2 %while.50 = (s32[]{:T(128)}, bf16[2,512,128]{2,1,0:T(8,128)(2,1)S(1)}, f32[256,1,3,128]{0,3,2,1:T(8,128)S(1)}, s32[]{:T(128)}, bf16[2,512,128]{2,1,0:T(8,128)(2,...) while((s32[]{:T(128)}, ...), condition=%wide.region_10.0_spmd.clone, body=%wide.region_7.10_spmd.clone.sunk | while | flops 253886976 | bytes 6900121 | solution.py:138
  23.5 1.7 %conditional.7 = (f32[256,1,3,128]{0,3,2,1:T(8,128)S(1)}, bf16[2,256,128]{2,1,0:T(8,128)(2,1)S(1)}) conditional(s32[]{:T(128)} %convert_element_type.78, () %tuple.108, (bf16[2,512,128]{2,1,0:T(8,128)(2,1)S(1)}, s32[]{:T(128)}, s32[]{:T(128)}, s32[]{:T(128)}, s32[512]{0:T(512)S(1)}, /*index=5*/s32[1,256]{1,0:T(1,128)S(1)}, ...), branch_computations={%region_8.8_spmd, %region_9.9_spmd} | conditional | flops 253690368 | bytes 5456986 | solution.py:121
  23.8 0.4 fusion.21
  24.1 0.3 fusion.22
  24.4 0.2 convolution_bitcast_fusion.2
  24.7 0.2 convolution_bitcast_fusion.3
  24.9 0.3 convolution_bitcast_fusion.4
  25.7 0.7 copy-done.2
  26.4 0.5 all-gather.3.cloned.1.call-update
  27.0 15.4 %reduce-scatter.3.cloned.1.call-done = bf16[2,256,128]{2,1,0:T(8,128)(2,1)} async-done(((bf16[2,512,128]{2,1,0:T(8,128)(2,1)}), bf16[2,256,128]{2,1,0:T(8,128)(2,1)}) %reduce-scatter.3.cloned.1.call-update) | async-done | bytes 131088 | tf_op jit(solution)/shard_map/reduce_scatter | solution.py:139
  42.5 27.0 %all-gather.3.cloned.1.call-done = bf16[1,256,3072]{2,1,0:T(8,128)(2,1)} async-done(((bf16[1,64,3072]{2,1,0:T(8,128)(2,1)}), bf16[1,256,3072]{2,1,0:T(8,128)(2,1)}) %all-gather.3.cloned.1.call-update) | async-done | bytes 1572880 | tf_op jit(solution)/shard_map/all_gather | solution.py:157
  69.4 2.8 %fusion.33 = bf16[3072,128]{0,1:T(8,128)(2,1)} fusion(bf16[1,256,3072]{2,1,0:T(8,128)(2,1)} %all-gather.3.cloned.1.call-done, bf16[2,256,128]{2,1,0:T(8,128)(2,1)} %reduce-scatter.3.cloned.1.call-done), kind=kOutput, calls=%fused_computation.59 | convolution fusion | flops 201719808 | bytes 2424832 | tf_op jit(solution)/shard_map/dot_general | solution.py:160
  72.3 1.3 fusion.34
  73.7 0.6 fusion.37
  74.2 0.5 copy-done.4
  74.7 1.8 %fusion.32 = bf16[256,3072]{1,0:T(8,128)(2,1)} fusion(f32[256,3072]{1,0:T(8,128)S(1)} %fusion.37, bf16[3072,128]{1,0:T(8,128)(2,1)S(1)} %copy-done.4, bf16[2,256,128]{2,1,0:T(8,128)(2,1)S(1)} %copy-done.5), kind=kOutput, calls=%fused_computation.56 | convolution fusion | flops 202899456 | bytes 5570560 | tf_op jit(solution)/shard_map/dot_general | solution.py:149
  76.6 0.8 copy.25
  77.4 54.3 %all-reduce.3.cloned.1.call-done = (bf16[3072,128]{0,1:T(8,128)(2,1)}, bf16[3072,128]{0,1:T(8,128)(2,1)}) async-done(((bf16[3072,128]{0,1:T(8,128)(2,1)}, bf16[3072,128]{0,1:T(8,128)(2,1)}), (bf16[3072,128]{0,1:T(8,128)(2,1)}, bf16[3072,128]{0,1:T(8,128)(2,1)})) %all-reduce.3.cloned.1.call-update) | async-done | bytes 1572880 | tf_op jit(solution)/shard_map/psum | solution.py:167
  131.7 2.6 %copy.26 = f32[3072,128]{1,0:T(8,128)} copy(bf16[3072,128]{0,1:T(8,128)(2,1)} %get-tuple-element.776) | data formatting | bytes 2359296
  134.3 1.4 copy.27
  (51 shorter events, 1.2 us)
Async XLA Ops:
  8.0 65.7 %copy-start = (bf16[3072,128]{1,0:T(8,128)(2,1)S(1)}, bf16[3072,128]{1,0:T(8,128)(2,1)}, u32[]{:S(2)}) copy-start(bf16[3072,128]{1,0:T(8,128)(2,1)} %param.22) | copy-start | bytes 2359300
  8.0 14.2 %copy-start.7 = (s32[1,256]{1,0:T(1,128)S(1)}, s32[1,256]{1,0:T(1,128)}, u32[]{:S(2)}) copy-start(s32[1,256]{1,0:T(1,128)} %param.20) | copy-start | bytes 3076
  8.0 13.9 %copy-start.6 = (bf16[1,256,384]{2,1,0:T(8,128)(2,1)S(1)}, bf16[1,256,384]{2,1,0:T(8,128)(2,1)}, u32[]{:S(2)}) copy-start(bf16[1,256,384]{2,1,0:T(8,128)(2,1)} %param.19) | copy-start | bytes 589828
  8.0 34.4 %reduce-scatter.3.cloned.1.call-start = ((), (), s32[]{:S(2)}) async-start(), calls=%async_computation.2 | async-start | bytes 393216 | tf_op jit(solution)/shard_map/reduce_scatter | solution.py:139
  25.7 0.7 copy-start.2
  26.4 43.1 %all-gather.3.cloned.1.call-start = ((), (), s32[]{:S(2)}) async-start(), calls=%async_computation.4 | async-start | bytes 1966080 | tf_op jit(solution)/shard_map/all_gather | solution.py:157
  27.0 104.7 %all-reduce.3.cloned.1.call-start = ((), (), s32[]{:S(2)}) async-start(), calls=%async_computation.5 | async-start | bytes 3145728 | tf_op jit(solution)/shard_map/psum | solution.py:167
  42.5 29.8 %copy-start.5 = (bf16[2,256,128]{2,1,0:T(8,128)(2,1)S(1)}, bf16[2,256,128]{2,1,0:T(8,128)(2,1)}, u32[]{:S(2)}) copy-start(bf16[2,256,128]{2,1,0:T(8,128)(2,1)} %reduce-scatter.3.cloned.1.call-done) | copy-start | bytes 393220
  69.4 2.9 %copy-start.1 = (bf16[1,256,3072]{2,1,0:T(8,128)(2,1)S(1)}, bf16[1,256,3072]{2,1,0:T(8,128)(2,1)}, u32[]{:S(2)}) copy-start(bf16[1,256,3072]{2,1,0:T(8,128)(2,1)} %all-gather.3.cloned.1.call-done) | copy-start | bytes 4718596
  73.6 1.1 copy-start.4
  73.6 62.1 %reduce-scatter.5.cloned.1.call-start = ((), (), s32[]{:S(2)}) async-start(), calls=%async_computation.3 | async-start | bytes 1966080 | tf_op jit(solution)/shard_map/reduce_scatter | solution.py:152
  131.6 2.6 %copy-start.3 = (bf16[3072,128]{0,1:T(8,128)(2,1)S(1)}, bf16[3072,128]{0,1:T(8,128)(2,1)}, u32[]{:S(2)}) copy-start(bf16[3072,128]{0,1:T(8,128)(2,1)} %get-tuple-element.777) | copy-start | bytes 2359300
Sparse Core Ops, SparseCore 0:
  26.5 15.9 reduce-scatter.2
  73.7 57.8 all-reduce.2
Sparse Core Ops, SparseCore 1:
  28.4 41.0 all-gather.2
  77.0 34.3 reduce-scatter.4
where the time goes:
time: 143 us
  waiting for transfers between devices  97.3 us (68%)
  between operations  15.7 us (11%)
  blocking collectives  11.6 us (8%)
  matrix products  8.42 us (6%)
  local copies, waits for them, and re-layouts  7.89 us (6%)
  other arithmetic  1.75 us (1%)
    psum x1, waiting for transfers between devices, shards(): lax.psum(key_part.astype(jnp.bfloat16), ('dp', 'seq')).astype(jnp.float32)  54.3 us
    all_gather x1, waiting for transfers between devices, shards(): input_piece = lax.all_gather(layer_input[0], 'head', axis=0, tiled=True)  27 us
    reduce_scatter x1, waiting for transfers between devices, shards(): lax.psum_scatter(grad_terms.astype(jnp.bfloat16), 'seq', scatter_dimensio...  15.4 us
    unnamed x23, local copies, waits for them, and re-layouts  7.6 us
    all_gather x1, blocking collectives, shards(): all_blocks = lax.all_gather(own_blocks, 'seq', axis=1, tiled=True)  7.12 us
    all_gather x1, blocking collectives, shards(): all_docs = lax.all_gather(doc_ids, 'seq', axis=1, tiled=True)[0]  4.44 us
  transfers between devices with their start and end apart: 4, of which 3 were waited for; matrix products, arithmetic and copies ran while one was open for 5% of the time, Pallas kernels for 0%

commit v1 on v0

--- a/solution.py
+++ b/solution.py
@@ -164,7 +164,9 @@
         input_piece, sub_grads[1], contract_rows, preferred_element_type=jnp.float32
     )
     grad_keyproj, grad_valueproj = (
-        lax.psum(key_part.astype(jnp.bfloat16), ("dp", "seq")).astype(jnp.float32),
+        jnp.sum(lax.all_gather(key_part.astype(jnp.bfloat16), ("dp", "seq")), axis=0).astype(
+            jnp.float32
+        ),
         lax.psum(value_part.astype(jnp.bfloat16), ("dp", "seq")).astype(jnp.float32),
     )
     return (query_grad, input_grad, grad_keyproj, grad_valueproj)

time: 143 us -> 195 us (1.36)
  waiting for transfers between devices: 97.3 us -> 138 us
  local copies, waits for them, and re-layouts: 7.89 us -> 14.6 us
  other arithmetic: 1.75 us -> 6.29 us
    all_gather x0 -> x1, waiting for transfers between devices: none -> 44.7 us  [shards(): lax.all_gather(key_part.astype(jnp.bfloat16), ('dp', 'seq'))]
    unnamed x23 -> x22, local copies, waits for them, and re-layouts: 7.6 us -> 14.3 us
    psum x1, waiting for transfers between devices: 54.3 us -> 49.6 us  [shards(): lax.psum(value_part.astype(jnp.bfloat16), ('dp', 'seq')).astype(jnp.float32)]
    reduce_sum x0 -> x1, other arithmetic: none -> 4.65 us  [shards(): jnp.sum(lax.all_gather(key_part.astype(jnp.bfloat16), ('dp', 'seq')), axi...]
  transfers between devices with their start and end apart: 4 -> 5, of which waited for: 3 -> 4; matrix products, arithmetic and copies ran while one was open for 5% -> 10% of each run, Pallas kernels for 0% -> 0%
where the time goes in v1:
time: 195 us; the launch traced here: 194 us
  waiting for transfers between devices  138 us (71%)
  between operations  15.4 us (8%)
  local copies, waits for them, and re-layouts  14.6 us (7%)
  blocking collectives  11.2 us (6%)
  matrix products  8.41 us (4%)
  other arithmetic  6.29 us (3%)
    psum x1, waiting for transfers between devices, shards(): lax.psum(value_part.astype(jnp.bfloat16), ('dp', 'seq')).astype(jnp.float32)  49.6 us
    all_gather x1, waiting for transfers between devices, shards(): lax.all_gather(key_part.astype(jnp.bfloat16), ('dp', 'seq'))  44.7 us
    all_gather x1, waiting for transfers between devices, shards(): input_piece = lax.all_gather(layer_input[0], 'head', axis=0, tiled=True)  27 us
    reduce_scatter x1, waiting for transfers between devices, shards(): lax.psum_scatter(grad_terms.astype(jnp.bfloat16), 'seq', scatter_dimensio...  15.7 us
    unnamed x22, local copies, waits for them, and re-layouts  14.3 us
    all_gather x1, blocking collectives, shards(): all_blocks = lax.all_gather(own_blocks, 'seq', axis=1, tiled=True)  5.64 us
    all_gather x1, blocking collectives, shards(): all_docs = lax.all_gather(doc_ids, 'seq', axis=1, tiled=True)[0]  5.58 us
    reduce_sum x1, other arithmetic, shards(): jnp.sum(lax.all_gather(key_part.astype(jnp.bfloat16), ('dp', 'seq')), axi...  4.65 us
  transfers between devices with their start and end apart: 5, of which 4 were waited for; matrix products, arithmetic and copies ran while one was open for 10% of the time, Pallas kernels for 0%

profile of v1, /device:TPU:0, one launch (start us, length us, event | category | flops | bytes accessed | tf_op | source)
XLA Modules:
  0.0 194.3 jit_solution(2653759818670461496)
XLA Ops:
  8.1 5.6 %all_gather.16 = s32[1,512]{1,0:T(1,128)S(1)} all-gather(s32[1,256]{1,0:T(1,128)} %param.20), channel_id=1, replica_groups=mesh['dp'=4,'seq'=2,'head'=4] {'seq'}, dimensions={1}, use_global_device_ids=true | all-gather | bytes 3072 | tf_op jit(solution)/shard_map/all_gather | solution.py:23
  13.7 0.9 pad_maximum_fusion.1
  14.6 5.6 %all_gather.15 = bf16[2,512,128]{2,1,0:T(8,128)(2,1)S(1)} all-gather(bf16[2,256,128]{2,1,0:T(8,128)(2,1)S(1)} %pad_maximum_fusion.1), channel_id=1, replica_groups=mesh['dp'=4,'seq'=2,'head'=4] {'seq'}, dimensions={1}, use_global_device_ids=true | all-gather | bytes 393216 | tf_op jit(solution)/shard_map/all_gather | solution.py:80
  20.2 1.1 copy.28
  21.8 1.2 while.49
  21.8 1.1 conditional.6
  22.1 0.3 fusion.38
  22.4 0.3 fusion.7
  23.0 2.2 %while.50 = (s32[]{:T(128)}, bf16[2,512,128]{2,1,0:T(8,128)(2,1)S(1)}, f32[256,1,3,128]{0,3,2,1:T(8,128)S(1)}, s32[]{:T(128)}, bf16[2,512,128]{2,1,0:T(8,128)(2,...) while((s32[]{:T(128)}, ...), condition=%wide.region_10.0_spmd.clone, body=%wide.region_7.10_spmd.clone.sunk | while | flops 253886976 | bytes 6900121 | solution.py:138
  23.1 1.7 conditional.7
  23.3 0.4 fusion.21
  23.7 0.3 convolution_bitcast_fusion.3
  24.0 0.3 fusion.22
  24.2 0.3 convolution_bitcast_fusion.4
  24.5 0.2 convolution_bitcast_fusion.2
  25.2 0.7 copy-done.2
  26.0 0.5 all-gather.5.cloned.1.call-update
  26.6 15.7 %reduce-scatter.3.cloned.1.call-done = bf16[2,256,128]{2,1,0:T(8,128)(2,1)} async-done(((bf16[2,512,128]{2,1,0:T(8,128)(2,1)}), bf16[2,256,128]{2,1,0:T(8,128)(2,1)}) %reduce-scatter.3.cloned.1.call-update) | async-done | bytes 131088 | tf_op jit(solution)/shard_map/reduce_scatter | solution.py:139
  42.3 27.0 %all-gather.5.cloned.1.call-done = bf16[1,256,3072]{2,1,0:T(8,128)(2,1)} async-done(((bf16[1,64,3072]{2,1,0:T(8,128)(2,1)}), bf16[1,256,3072]{2,1,0:T(8,128)(2,1)}) %all-gather.5.cloned.1.call-update) | async-done | bytes 1572880 | tf_op jit(solution)/shard_map/all_gather | solution.py:157
  69.3 2.8 %fusion.34 = bf16[3072,128]{0,1:T(8,128)(2,1)} fusion(bf16[1,256,3072]{2,1,0:T(8,128)(2,1)} %all-gather.5.cloned.1.call-done, bf16[2,256,128]{2,1,0:T(8,128)(2,1)} %reduce-scatter.3.cloned.1.call-done), kind=kOutput, calls=%fused_computation.61 | convolution fusion | flops 201719808 | bytes 2424832 | tf_op jit(solution)/shard_map/dot_general | solution.py:163
  72.2 1.3 fusion.33
  73.5 0.2 reduce-scatter.5.cloned.1.call-start
  73.8 0.6 fusion.37
  74.4 0.3 copy-done.3
  74.7 1.7 fusion.32
  76.4 0.8 copy.34
  77.3 49.6 %all-reduce.2.cloned.1.call-done = bf16[3072,128]{0,1:T(8,128)(2,1)} async-done(((bf16[3072,128]{0,1:T(8,128)(2,1)}), bf16[3072,128]{0,1:T(8,128)(2,1)}) %all-reduce.2.cloned.1.call-update) | async-done | bytes 786448 | tf_op jit(solution)/shard_map/psum | solution.py:170
  126.9 2.5 %copy.36 = f32[3072,128]{1,0:T(8,128)} copy(bf16[3072,128]{0,1:T(8,128)(2,1)} %all-reduce.2.cloned.1.call-done) | data formatting | bytes 2359296
  129.4 44.7 %all-gather.7.cloned.1.call-done = bf16[24576,128]{0,1:T(8,128)(2,1)} async-done(((bf16[3072,128]{0,1:T(8,128)(2,1)}), bf16[24576,128]{0,1:T(8,128)(2,1)}) %all-gather.7.cloned.1.call-update) | async-done | bytes 6291472 | tf_op jit(solution)/shard_map/all_gather | solution.py:167
  174.1 7.0 %copy.40 = bf16[16,8,8,3072]{3,2,1,0:T(8,128)(2,1)S(1)} copy(bf16[16,8,8,3072]{3,1,2,0:T(8,128)(2,1)} %bitcast.150) | data formatting | bytes 12582912
  181.1 4.6 %bitcast_reduce_fusion = bf16[3072,128]{0,1:T(8,128)(2,1)S(1)} fusion(bf16[16,8,8,3072]{3,2,1,0:T(8,128)(2,1)S(1)} %copy.40), kind=kLoop, calls=%fused_computation.55 | loop fusion | flops 2752512 | bytes 7077888 | tf_op jit(solution)/shard_map/reduce_sum | solution.py:167
  185.7 1.4 copy.35
  (54 shorter events, 1.9 us)
Async XLA Ops:
  8.0 65.8 %copy-start = (bf16[3072,128]{1,0:T(8,128)(2,1)S(1)}, bf16[3072,128]{1,0:T(8,128)(2,1)}, u32[]{:S(2)}) copy-start(bf16[3072,128]{1,0:T(8,128)(2,1)} %param.22) | copy-start | bytes 2359300
  8.0 13.8 %copy-start.6 = (s32[1,256]{1,0:T(1,128)S(1)}, s32[1,256]{1,0:T(1,128)}, u32[]{:S(2)}) copy-start(s32[1,256]{1,0:T(1,128)} %param.20) | copy-start | bytes 3076
  8.0 13.4 %copy-start.5 = (bf16[1,256,384]{2,1,0:T(8,128)(2,1)S(1)}, bf16[1,256,384]{2,1,0:T(8,128)(2,1)}, u32[]{:S(2)}) copy-start(bf16[1,256,384]{2,1,0:T(8,128)(2,1)} %param.19) | copy-start | bytes 589828
  8.0 34.2 %reduce-scatter.3.cloned.1.call-start = ((), (), s32[]{:S(2)}) async-start(), calls=%async_computation.2 | async-start | bytes 393216 | tf_op jit(solution)/shard_map/reduce_scatter | solution.py:139
  25.2 0.7 copy-start.2
  26.0 43.3 %all-gather.5.cloned.1.call-start = ((), (), s32[]{:S(2)}) async-start(), calls=%async_computation.5 | async-start | bytes 1966080 | tf_op jit(solution)/shard_map/all_gather | solution.py:157
  26.5 100.4 %all-reduce.2.cloned.1.call-start = ((), (), s32[]{:S(2)}) async-start(), calls=%async_computation.4 | async-start | bytes 1572864 | tf_op jit(solution)/shard_map/psum | solution.py:170
  42.3 29.9 %copy-start.4 = (bf16[2,256,128]{2,1,0:T(8,128)(2,1)S(1)}, bf16[2,256,128]{2,1,0:T(8,128)(2,1)}, u32[]{:S(2)}) copy-start(bf16[2,256,128]{2,1,0:T(8,128)(2,1)} %reduce-scatter.3.cloned.1.call-done) | copy-start | bytes 393220
  69.3 2.9 %copy-start.1 = (bf16[1,256,3072]{2,1,0:T(8,128)(2,1)S(1)}, bf16[1,256,3072]{2,1,0:T(8,128)(2,1)}, u32[]{:S(2)}) copy-start(bf16[1,256,3072]{2,1,0:T(8,128)(2,1)} %all-gather.5.cloned.1.call-done) | copy-start | bytes 4718596
  72.1 102.0 %all-gather.7.cloned.1.call-start = ((), (), s32[]{:S(2)}) async-start(), calls=%async_computation.6 | async-start | bytes 7077888 | tf_op jit(solution)/shard_map/all_gather | solution.py:167
  73.5 1.1 copy-start.3
  73.5 113.6 %reduce-scatter.5.cloned.1.call-start = ((), (), s32[]{:S(2)}) async-start(), calls=%async_computation.3 | async-start | bytes 1966080 | tf_op jit(solution)/shard_map/reduce_scatter | solution.py:152
Sparse Core Ops, SparseCore 0:
  26.1 16.1 reduce-scatter.2
  72.3 54.5 all-reduce.1
  129.4 44.6 all-gather.6
Sparse Core Ops, SparseCore 1:
  28.0 41.2 all-gather.4
  76.9 34.3 reduce-scatter.4
